TPU v7x, 32 devices: a whole 2x2x4 slice. The times are simulated.
32 devices in a mesh: dp: 8 (over y, x, core), tensor: 4 (over z).
Axes of the slice: x: 2, y: 2, z: 4, core: 2. Of those that a mesh axis runs over, the one named last changes fastest.
Arguments:
- images: bfloat16 [32, 320, 1024], P('dp', None, 'tensor'), may hold values from -6 to 6
- lengths: int32 [32], P('dp'), may hold values from 224 to 320, as said below
- cotangent: bfloat16 [32, 320, 1024], P('dp', None, 'tensor'), may hold values from -6 to 6
- norm1_gain: float32 [1024], replicated, may hold values from 0.5 to 1.5
- norm1_shift: float32 [1024], replicated, may hold values from -1.75 to 1.75
- w_qkv: bfloat16 [1024, 3, 1024], P(None, None, 'tensor'), may hold values from -0.1875 to 0.1875
- qv_bias: float32 [2, 1024], P(None, 'tensor'), may hold values from -3 to 3
- w_proj: bfloat16 [1024, 1024], P('tensor'), may hold values from -1.5 to 1.5
- proj_bias: float32 [1024], replicated, may hold values from -3 to 3
- norm2_gain: float32 [1024], replicated, may hold values from 0.5 to 1.5
- norm2_shift: float32 [1024], replicated, may hold values from -1.75 to 1.75
- w_fc1: bfloat16 [1024, 4096], P(None, 'tensor'), may hold values from -0.1875 to 0.1875
- fc1_bias: float32 [4096], P('tensor'), may hold values from -3 to 3
- w_fc2: bfloat16 [4096, 1024], P('tensor'), may hold values from -0.09375 to 0.09375
- fc2_bias: float32 [1024], replicated, may hold values from -3 to 3
Outputs:
- output: bfloat16 [32, 320, 1024], P('dp', None, 'tensor')
- input_grad: bfloat16 [32, 320, 1024], P('dp', None, 'tensor')
- grad_norm1_gain: float32 [1024], replicated
- grad_norm1_shift: float32 [1024], replicated
- grad_w_qkv: float32 [1024, 3, 1024], P(None, None, 'tensor')
- grad_qv_bias: float32 [2, 1024], P(None, 'tensor')
- grad_w_proj: float32 [1024, 1024], P('tensor')
- grad_proj_bias: float32 [1024], replicated
- grad_norm2_gain: float32 [1024], replicated
- grad_norm2_shift: float32 [1024], replicated
- grad_w_fc1: float32 [1024, 4096], P(None, 'tensor')
- grad_fc1_bias: float32 [4096], P('tensor')
- grad_w_fc2: float32 [4096, 1024], P('tensor')
- grad_fc2_bias: float32 [1024], replicated
Inputs may be any that keep to these rules, and one draw needn't show every extreme that they name: lengths[i] is the number of valid slots of image i, which come first; some image has all 320 slots valid in every draw.
All inputs are finite; a program needn't handle non-finite values.
Results may differ from a plain program's by a relative error of at most 0.02.
Values may be sent and summed in bfloat16 or wider, within the bound.
A program may use at most 192 MiB of HBM per device.

v0:
```python
import jax
import jax.numpy as jnp
from jax import lax
from jax.sharding import PartitionSpec as P

HEAD_DIM = 64
EPS = 1e-06
MASKED = -1e30


def norm_rows(values, gain_row, shift_row):
    row_mean = jnp.mean(values, axis=-1, keepdims=True)
    centered = values - row_mean
    spread = jnp.mean(centered * centered, axis=-1, keepdims=True)
    inverse = lax.rsqrt(spread + EPS)
    unit_rows = centered * inverse
    return (unit_rows * gain_row + shift_row, unit_rows, inverse)


def norm_back(gradient, unit_rows, inverse, gain_row):
    scaled = gradient * gain_row
    first_mean = jnp.mean(scaled, axis=-1, keepdims=True)
    cross_mean = jnp.mean(scaled * unit_rows, axis=-1, keepdims=True)
    return inverse * (scaled - first_mean - unit_rows * cross_mean)


def scores_of(queries, key_heads, key_mask, score_scale):
    raw_scores = (
        jnp.einsum("bqhe,bkhe->bhqk", queries, key_heads, preferred_element_type=jnp.float32)
        * score_scale
    )
    return jnp.where(key_mask, raw_scores, MASKED)


def exact_gelu(values):
    return jax.nn.gelu(values, approximate=False)


def per_device(
    images,
    lengths,
    cotangent,
    norm1_gain,
    norm1_shift,
    w_qkv,
    qv_bias,
    w_proj,
    proj_bias,
    norm2_gain,
    norm2_shift,
    w_fc1,
    fc1_bias,
    w_fc2,
    fc2_bias,
):
    images_here, slot_count, col_count = images.shape
    model_width = w_qkv.shape[0]
    local_width = w_qkv.shape[2]
    heads_here = local_width // HEAD_DIM
    row_count = images_here * slot_count
    score_scale = HEAD_DIM ** (-0.5)
    first_col = lax.axis_index("tensor") * col_count
    full_images, full_cot = (
        lax.all_gather(images, "tensor", axis=2, tiled=True),
        lax.all_gather(cotangent, "tensor", axis=2, tiled=True),
    )
    slot_ids = jnp.arange(slot_count, dtype=jnp.int32)
    valid_slots = (slot_ids[None, :] < lengths[:, None]).astype(jnp.float32)
    keep_rows = valid_slots.reshape(row_count, 1)
    row_values = full_images.reshape(row_count, model_width).astype(jnp.float32) * keep_rows
    normed1, unit1, inverse1 = norm_rows(row_values, norm1_gain, norm1_shift)
    normed1 = normed1.astype(jnp.bfloat16)
    qkv_bias = jnp.concatenate([qv_bias[0], jnp.zeros_like(qv_bias[0]), qv_bias[1]])
    w_flat = w_qkv.reshape(model_width, 3 * local_width)
    qkv_rows = (jnp.dot(normed1, w_flat, preferred_element_type=jnp.float32) + qkv_bias).astype(
        jnp.bfloat16
    )
    qkv_rows = qkv_rows.reshape(images_here, slot_count, 3, heads_here, HEAD_DIM)
    queries = qkv_rows[:, :, 0]
    key_heads = qkv_rows[:, :, 1]
    value_heads = qkv_rows[:, :, 2]
    key_mask = valid_slots[:, None, None, :] > 0
    scores = scores_of(queries, key_heads, key_mask, score_scale)
    row_top = jnp.max(scores, axis=-1, keepdims=True)
    shifted = jnp.exp(scores - row_top)
    row_total = jnp.sum(shifted, axis=-1, keepdims=True)
    probability = (shifted / row_total).astype(jnp.bfloat16)
    log_total = row_top + jnp.log(row_total)
    mixed = jnp.einsum(
        "bhqk,bkhe->bqhe", probability, value_heads, preferred_element_type=jnp.float32
    ).astype(jnp.bfloat16)
    mixed_rows = mixed.reshape(row_count, local_width)
    attn_part = jnp.dot(mixed_rows, w_proj, preferred_element_type=jnp.float32)
    middle = (
        row_values
        + lax.psum(attn_part.astype(jnp.bfloat16), "tensor").astype(jnp.float32)
        + proj_bias
    )
    normed2, unit2, inverse2 = norm_rows(middle, norm2_gain, norm2_shift)
    normed2 = normed2.astype(jnp.bfloat16)
    pre_act = jnp.dot(normed2, w_fc1, preferred_element_type=jnp.float32) + fc1_bias
    activated = exact_gelu(pre_act).astype(jnp.bfloat16)
    ff_part = jnp.dot(activated, w_fc2, preferred_element_type=jnp.float32)
    ff_share = lax.psum_scatter(
        ff_part.astype(jnp.bfloat16), "tensor", scatter_dimension=1, tiled=True
    ).astype(jnp.float32)
    middle_cols = lax.dynamic_slice_in_dim(middle, first_col, col_count, 1)
    bias_cols = lax.dynamic_slice_in_dim(fc2_bias, first_col, col_count, 0)
    output = ((middle_cols + ff_share + bias_cols) * keep_rows).astype(jnp.bfloat16)
    output = output.reshape(images_here, slot_count, col_count)
    grad_out = full_cot.reshape(row_count, model_width).astype(jnp.float32) * keep_rows
    grad_ff = grad_out.astype(jnp.bfloat16)
    grad_fc2_bias = jnp.sum(grad_ff, axis=0, dtype=jnp.float32)
    grad_w_fc2 = jnp.einsum("rf,rd->fd", activated, grad_ff, preferred_element_type=jnp.float32)
    grad_act = jnp.einsum("rd,fd->rf", grad_ff, w_fc2, preferred_element_type=jnp.float32)
    gelu_pull = jax.vjp(exact_gelu, pre_act)[1]
    grad_pre = gelu_pull(grad_act)[0].astype(jnp.bfloat16)
    grad_fc1_bias = jnp.sum(grad_pre, axis=0, dtype=jnp.float32)
    grad_w_fc1 = jnp.einsum("rd,rf->df", normed2, grad_pre, preferred_element_type=jnp.float32)
    hidden_part = jnp.einsum("rf,df->rd", grad_pre, w_fc1, preferred_element_type=jnp.float32)
    grad_normed2 = lax.psum(hidden_part.astype(jnp.bfloat16), "tensor").astype(jnp.float32)
    grad_norm2_gain = jnp.sum(grad_normed2 * unit2, axis=0)
    grad_norm2_shift = jnp.sum(grad_normed2, axis=0)
    grad_middle = grad_out + norm_back(grad_normed2, unit2, inverse2, norm2_gain)
    grad_attn = grad_middle.astype(jnp.bfloat16)
    grad_proj_bias = jnp.sum(grad_attn, axis=0, dtype=jnp.float32)
    grad_w_proj = jnp.einsum("rc,rd->cd", mixed_rows, grad_attn, preferred_element_type=jnp.float32)
    grad_mixed = jnp.einsum(
        "rd,cd->rc", grad_attn, w_proj, preferred_element_type=jnp.float32
    ).astype(jnp.bfloat16)
    grad_mixed = grad_mixed.reshape(images_here, slot_count, heads_here, HEAD_DIM)
    scores_again = scores_of(queries, key_heads, key_mask, score_scale)
    weights_soft = jnp.exp(scores_again - log_total)
    grad_value = jnp.einsum(
        "bhqk,bqhe->bkhe",
        weights_soft.astype(jnp.bfloat16),
        grad_mixed,
        preferred_element_type=jnp.float32,
    )
    grad_prob = jnp.einsum(
        "bqhe,bkhe->bhqk", grad_mixed, value_heads, preferred_element_type=jnp.float32
    )
    row_dot = jnp.sum(weights_soft * grad_prob, axis=-1, keepdims=True)
    grad_scores = (weights_soft * (grad_prob - row_dot)).astype(jnp.bfloat16)
    grad_query = (
        jnp.einsum("bhqk,bkhe->bqhe", grad_scores, key_heads, preferred_element_type=jnp.float32)
        * score_scale
    )
    grad_key = (
        jnp.einsum("bhqk,bqhe->bkhe", grad_scores, queries, preferred_element_type=jnp.float32)
        * score_scale
    )
    grad_qkv = jnp.stack([grad_query, grad_key, grad_value], axis=2).astype(jnp.bfloat16)
    grad_qkv = grad_qkv.reshape(row_count, 3 * local_width)
    bias_sums = jnp.sum(grad_qkv, axis=0, dtype=jnp.float32).reshape(3, local_width)
    grad_qv_bias = jnp.stack([bias_sums[0], bias_sums[2]])
    grad_w_qkv = jnp.einsum("rd,rc->dc", normed1, grad_qkv, preferred_element_type=jnp.float32)
    grad_w_qkv = grad_w_qkv.reshape(model_width, 3, local_width)
    normed_part = jnp.einsum("rc,dc->rd", grad_qkv, w_flat, preferred_element_type=jnp.float32)
    grad_normed1 = lax.psum(normed_part.astype(jnp.bfloat16), "tensor").astype(jnp.float32)
    grad_norm1_gain = jnp.sum(grad_normed1 * unit1, axis=0)
    grad_norm1_shift = jnp.sum(grad_normed1, axis=0)
    grad_full = grad_middle + norm_back(grad_normed1, unit1, inverse1, norm1_gain)
    grad_input = lax.dynamic_slice_in_dim(grad_full, first_col, col_count, 1) * keep_rows
    input_grad = grad_input.astype(jnp.bfloat16).reshape(images_here, slot_count, col_count)
    summed = (
        lax.psum(grad_norm1_gain.astype(jnp.bfloat16), "dp").astype(jnp.float32),
        lax.psum(grad_norm1_shift.astype(jnp.bfloat16), "dp").astype(jnp.float32),
        lax.psum(grad_w_qkv.astype(jnp.bfloat16), "dp").astype(jnp.float32),
        lax.psum(grad_qv_bias.astype(jnp.bfloat16), "dp").astype(jnp.float32),
        lax.psum(grad_w_proj.astype(jnp.bfloat16), "dp").astype(jnp.float32),
        lax.psum(grad_proj_bias.astype(jnp.bfloat16), "dp").astype(jnp.float32),
        lax.psum(grad_norm2_gain.astype(jnp.bfloat16), "dp").astype(jnp.float32),
        lax.psum(grad_norm2_shift.astype(jnp.bfloat16), "dp").astype(jnp.float32),
        lax.psum(grad_w_fc1.astype(jnp.bfloat16), "dp").astype(jnp.float32),
        lax.psum(grad_fc1_bias.astype(jnp.bfloat16), "dp").astype(jnp.float32),
        lax.psum(grad_w_fc2.astype(jnp.bfloat16), "dp").astype(jnp.float32),
        lax.psum(grad_fc2_bias.astype(jnp.bfloat16), "dp").astype(jnp.float32),
    )
    return (
        output,
        input_grad,
        summed[0],
        summed[1],
        summed[2],
        summed[3],
        summed[4],
        summed[5],
        summed[6],
        summed[7],
        summed[8],
        summed[9],
        summed[10],
        summed[11],
    )


def solution(mesh):
    in_specs = (
        P("dp", None, "tensor"),
        P("dp"),
        P("dp", None, "tensor"),
        P(),
        P(),
        P(None, None, "tensor"),
        P(None, "tensor"),
        P("tensor", None),
        P(),
        P(),
        P(),
        P(None, "tensor"),
        P("tensor"),
        P("tensor", None),
        P(),
    )
    out_specs = (
        P("dp", None, "tensor"),
        P("dp", None, "tensor"),
        P(),
        P(),
        P(None, None, "tensor"),
        P(None, "tensor"),
        P("tensor", None),
        P(),
        P(),
        P(),
        P(None, "tensor"),
        P("tensor"),
        P("tensor", None),
        P(),
    )
    return jax.shard_map(
        per_device, mesh=mesh, in_specs=in_specs, out_specs=out_specs, check_vma=False
    )
```

profile of v0, /device:TPU:0, one launch (start us, length us, event | category | flops | bytes accessed | tf_op | source)
XLA Modules:
  0.0 699.4 jit_solution(9213317824829638723)
XLA Ops:
  8.7 0.8 fusion.59
  10.2 2.6 copy.39
  12.8 54.3 %all-gather.3.cloned.1.call-done = bf16[4,320,1024]{2,1,0:T(8,128)(2,1)} async-done(((bf16[4,320,256]{2,1,0:T(8,128)(2,1)}), bf16[4,320,1024]{2,1,0:T(8,128)(2,1)}) %all-gather.3.cloned.1.call-update) | async-done | bytes 2621456 | tf_op jit(solution)/shard_map/all_gather | solution.py:64
  67.2 2.6 fusion.18
  69.8 2.8 multiply_reduce_fusion.3
  72.6 1.3 add_convert_fusion.2
  73.9 1.5 copy-done.13
  75.4 3.5 add_convert_fusion.3
  78.9 6.7 reshape.265
  85.6 4.0 fusion.57
  89.6 2.3 copy.64
  91.8 2.5 copy.65
  94.3 3.2 copy.66
  97.5 3.2 fusion.24
  100.8 1.9 fusion
  102.7 2.4 fusion.35
  105.2 1.5 copy.45
  106.7 2.0 reshape.257
  108.7 3.4 convolution_convert_fusion.1
  112.3 9.5 %all-gather.5.cloned.1.call-done = bf16[4,320,1024]{2,1,0:T(8,128)(2,1)} async-done(((bf16[4,320,256]{2,1,0:T(8,128)(2,1)}), bf16[4,320,1024]{2,1,0:T(8,128)(2,1)}) %all-gather.5.cloned.1.call-update) | async-done | bytes 2621456 | tf_op jit(solution)/shard_map/all_gather | solution.py:65
  121.8 105.2 %all-reduce.7.cloned.1.call-done = bf16[1280,1024]{1,0:T(8,128)(2,1)} async-done(((bf16[1280,1024]{1,0:T(8,128)(2,1)}), bf16[1280,1024]{1,0:T(8,128)(2,1)}) %all-reduce.7.cloned.1.call-update) | async-done | bytes 2621456 | tf_op jit(solution)/shard_map/psum | solution.py:96
  227.0 5.0 fusion.56
  232.8 2.5 copy-done.48
  235.3 3.0 fusion.51
  238.4 16.8 %fusion.52 = (bf16[1024]{0:T(1024)(128)(2,1)}, bf16[1280,1024]{1,0:T(8,128)(2,1)S(1)}, f32[1280,1024]{1,0:T(8,128)}) fusion(f32[1280,1024]{1,0:T(8,128)S(1)} %fusion.51, f32[1024]{0:T(1024)S(1)} %copy-done.45, bf16[1280,1024]{1,0:T(8,128)(2,1)S(1)} %get-tuple-element.49, bf16[1024,1024]{1,0:T(8,128)(2,1)S(1)} %copy-done), kind=kOutput, calls=%fused_computation.113 | convolution fusion | flops 2781346816 | bytes 17831936 | tf_op jit(solution)/shard_map/rd,fd->rf/dot_general | solution.py:115
  255.2 1.5 copy-done.51
  256.6 4.2 convolution_convert_fusion.2
  260.9 1.4 log_add_fusion
  262.3 101.8 %all-reduce.9.cloned.1.call-done = bf16[1280,1024]{1,0:T(8,128)(2,1)} async-done(((bf16[1280,1024]{1,0:T(8,128)(2,1)}), bf16[1280,1024]{1,0:T(8,128)(2,1)}) %all-reduce.9.cloned.1.call-update) | async-done | bytes 2621456 | tf_op jit(solution)/shard_map/psum | solution.py:121
  364.1 5.5 fusion.9
  369.6 5.6 convert_reduce_fusion
  375.2 2.3 copy-done.4
  377.5 1.7 convolution_convert_fusion.4
  379.2 3.1 reshape.266
  382.3 3.2 copy.47
  385.5 5.5 fusion.27
  391.1 5.4 multiply_reduce_fusion
  396.5 2.9 multiply_convert_fusion
  399.4 1.3 multiply_bitcast_fusion
  400.8 0.9 multiply_bitcast_fusion.1
  402.2 3.2 copy.52
  405.5 4.7 convert_element_type.226
  410.2 5.7 convolution_convert_fusion
  416.0 5.5 multiply_convert_fusion.2
  421.5 1.5 copy-done.15
  423.0 4.1 convolution_convert_fusion.3
  427.4 7.1 %convolution_convert_fusion.5 = bf16[1024,1024]{1,0:T(8,128)(2,1)} fusion(bf16[1280,1024]{1,0:T(8,128)(2,1)} %copy-done.15, bf16[1280,1024]{1,0:T(8,128)(2,1)} %copy-done.12), kind=kOutput, calls=%fused_computation.66 | convolution fusion | flops 2685403136 | bytes 7340032 | tf_op jit(solution)/shard_map/rf,rd->fd/dot_general | solution.py:114
  434.5 7.3 %convolution_convert_fusion.6 = bf16[1024,1024]{1,0:T(8,128)(2,1)} fusion(bf16[1280,1024]{1,0:T(8,128)(2,1)S(1)} %copy-done.52, f32[1280,1024]{1,0:T(8,128)} %copy-done.2, f32[1024]{0:T(1024)S(1)} %copy-done.50, f32[1024]{0:T(1024)S(1)} %copy-done.38, f32[1280]{0:T(1024)S(1)} %copy-done.31, f32[1280]{0:T(1024)S(1)} %copy-done.25), kind=kOutput, calls=%fused_computation.67 | convolution fusion | flops 2691956736 | bytes 9979904 | tf_op jit(solution)/shard_map/rd,rf->df/dot_general | solution.py:119
  441.8 1.6 convolution_convert_fusion.8
  443.6 0.8 copy-done.19
  444.4 3.4 convolution_convert_fusion.7
  447.8 0.8 dynamic_slice.10
  448.8 2.3 fusion.25
  451.3 67.9 %all-reduce.11.cloned.1.call-done = bf16[1280,1024]{1,0:T(8,128)(2,1)} async-done(((bf16[1280,1024]{1,0:T(8,128)(2,1)}), bf16[1280,1024]{1,0:T(8,128)(2,1)}) %all-reduce.11.cloned.1.call-update) | async-done | bytes 2621456 | tf_op jit(solution)/shard_map/psum | solution.py:160
  519.2 2.2 reduce_sum.188
  521.4 7.4 %fusion.10 = (bf16[1024]{0:T(1024)(128)(2,1)S(1)}, f32[1280]{0:T(1024)S(1)}, f32[1280]{0:T(1024)S(1)}, f32[1280,1024]{1,0:T(8,128)}, f32[1280,1024]{1,0:T(8,128)}) fusion(bf16[1280,1024]{1,0:T(8,128)(2,1)} %all-reduce.11.cloned.1.call-done, f32[1280]{0:T(1024)S(1)} %rsqrt.22, f32[1280]{0:T(1024)S(1)} %div.43, f32[1280]{0:T(1024)S(1)} %reshape.262, ...), kind=kLoop, calls=%fused_computation.21 | loop fusion | flops 14414336 | bytes 15760384 | tf_op jit(solution)/shard_map/reduce_sum | solution.py:161
  528.9 24.7 %all-reduce = (bf16[1024]{0:T(1024)(128)(2,1)S(1)}, bf16[1024]{0:T(1024)(128)(2,1)S(1)}, bf16[2,256]{1,0:T(2,128)(2,1)S(1)}, bf16[1024]{0:T(1024)(128)(2,1)S(1)}...) all-reduce(bf16[1024]{0:T(1024)(128)(2,1)S(1)} %get-tuple-element.1, ...), channel_id=1, replica_groups=mesh['dp'=8,'tensor'=4] {'dp'}, use_global_device_ids=true, to_apply=%region_16.17 | all-reduce | flops 7680 | bytes 30720 | tf_op jit(solution)/shard_map/psum | solution.py:167
  558.3 14.9 %reduce-scatter.2.cloned.1.call-done = bf16[1280,256]{1,0:T(8,128)(2,1)} async-done(((bf16[1280,1024]{1,0:T(8,128)(2,1)}), bf16[1280,256]{1,0:T(8,128)(2,1)}) %reduce-scatter.2.cloned.1.call-update) | async-done | bytes 655376 | tf_op jit(solution)/shard_map/reduce_scatter | solution.py:104
  573.2 4.1 fusion.32
  577.3 104.3 %all-reduce.13.cloned.1.call-done = (bf16[1024,3,256]{2,0,1:T(8,128)(2,1)}, bf16[256,1024]{1,0:T(8,128)(2,1)}, bf16[1024,1024]{1,0:T(8,128)(2,1)}, bf16[1024,1024]{1,0:T(8,128)(2,1)}) async-done(((bf16[1024,3,256]{2,0,1:T(8,128)(2,1)}, bf16[256,1024]{1,0:T(8,128)(2,1)}, bf16[1024,1024]{1,0:T(8,128)(2,1)}, bf16[1024,1024]{1,0:T(8,128)(2,1)}), (bf16[1024,3,256]{2,0,1:T(8,128)(2,1)}, ...) | async-done | bytes 6291472 | tf_op jit(solution)/shard_map/psum | solution.py:169
  681.6 2.3 convert_element_type.238
  683.9 3.5 convert_element_type.234
  687.4 2.5 convert_element_type.244
  689.8 2.5 convert_element_type.247
  (151 shorter events, 9.4 us)
Async XLA Ops:
  7.2 231.2 %copy-start = (bf16[1024,1024]{1,0:T(8,128)(2,1)S(1)}, bf16[1024,1024]{1,0:T(8,128)(2,1)}, u32[]{:S(2)}) copy-start(bf16[1024,1024]{1,0:T(8,128)(2,1)} %param.28) | copy-start | bytes 6291460
  7.2 65.4 %copy-start.39 = (f32[1024]{0:T(1024)S(1)}, f32[1024]{0:T(1024)}, u32[]{:S(2)}) copy-start(f32[1024]{0:T(1024)} %param.18) | copy-start | bytes 12292
  7.2 65.3 %copy-start.44 = (f32[1024]{0:T(1024)S(1)}, f32[1024]{0:T(1024)}, u32[]{:S(2)}) copy-start(f32[1024]{0:T(1024)} %param.19) | copy-start | bytes 12292
  7.2 60.0 %all-gather.3.cloned.1.call-start = ((), (), s32[]{:S(2)}) async-start(), calls=%async_computation.1 | async-start | bytes 3276800 | tf_op jit(solution)/shard_map/all_gather | solution.py:64
  8.0 113.8 %all-gather.5.cloned.1.call-start = ((), (), s32[]{:S(2)}) async-start(), calls=%async_computation.4 | async-start | bytes 3276800 | tf_op jit(solution)/shard_map/all_gather | solution.py:65
  8.7 218.3 %all-reduce.7.cloned.1.call-start = ((), (), s32[]{:S(2)}) async-start(), calls=%async_computation.2 | async-start | bytes 5242880 | tf_op jit(solution)/shard_map/psum | solution.py:96
  10.2 92.5 %copy-start.34 = (pred[4,320]{1,0:T(4,128)(4,1)}, pred[4,320]{1,0:T(4,128)(4,1)S(1)}, u32[]{:S(2)}) copy-start(pred[4,320]{1,0:T(4,128)(4,1)S(1)} %get-tuple-element.54) | copy-start | bytes 3844
  67.2 5.4 copy-start.3
  67.2 8.2 %copy-start.20 = (bf16[1024,3,256]{0,2,1:T(8,128)(2,1)S(1)}, bf16[1024,3,256]{0,2,1:T(8,128)(2,1)}, u32[]{:S(2)}) copy-start(bf16[1024,3,256]{0,2,1:T(8,128)(2,1)} %copy.39) | copy-start | bytes 4718596
  69.7 4.1 copy-start.26
  72.6 1.3 copy-start.32
  73.9 1.5 copy-start.13
  100.7 4.4 copy-start.1
  100.8 4.4 copy-start.22
  100.8 1.9 copy-start.9
  102.7 2.5 copy-start.28
  112.2 251.9 %all-reduce.9.cloned.1.call-start = ((), (), s32[]{:S(2)}) async-start(), calls=%async_computation.5 | async-start | bytes 5242880 | tf_op jit(solution)/shard_map/psum | solution.py:121
  232.0 6.3 copy-start.2
  232.0 6.3 copy-start.12
  232.0 0.7 copy-start.36
  232.0 3.2 copy-start.48
  232.0 3.2 copy-start.49
  232.1 6.2 copy-start.23
  235.3 3.1 copy-start.29
  235.3 3.1 copy-start.45
  238.3 16.8 %copy-start.8 = (f32[1280,1024]{1,0:T(8,128)}, f32[1280,1024]{1,0:T(8,128)S(1)}, u32[]{:S(2)}) copy-start(f32[1280,1024]{1,0:T(8,128)S(1)} %fusion.51) | copy-start | bytes 15728644
  255.2 1.5 copy-start.51
  260.9 258.3 %all-reduce.11.cloned.1.call-start = ((), (), s32[]{:S(2)}) async-start(), calls=%async_computation.6 | async-start | bytes 5242880 | tf_op jit(solution)/shard_map/psum | solution.py:160
  364.1 5.5 copy-start.5
  364.1 5.5 copy-start.6
  364.1 5.5 copy-start.24
  364.1 5.5 copy-start.30
  364.1 5.5 copy-start.37
  369.6 7.8 %copy-start.18 = (bf16[256,1024]{1,0:T(8,128)(2,1)S(1)}, bf16[256,1024]{1,0:T(8,128)(2,1)}, u32[]{:S(2)}) copy-start(bf16[256,1024]{1,0:T(8,128)(2,1)} %param.22) | copy-start | bytes 1572868
  375.2 2.3 copy-start.4
  385.5 5.5 copy-start.10
  385.5 5.6 copy-start.11
  385.5 5.6 copy-start.21
  385.5 5.6 copy-start.35
  385.5 11.0 %slice-start = ((s8[7864320]{0:T(1024)(128)(4,1)}), s8[4194304]{0:T(1024)(128)(4,1)S(1)}, s32[]{:S(2)}) async-start(s8[7864320]{0:T(1024)(128)(4,1)} %bitcast.95), calls=%async_computation.8 | async-start | bytes 8388608
  391.1 5.4 slice-start.1
  399.4 1.3 copy-start.7
  410.2 5.8 copy-start.46
  415.9 157.3 %reduce-scatter.2.cloned.1.call-start = ((), (), s32[]{:S(2)}) async-start(), calls=%async_computation.3 | async-start | bytes 3276800 | tf_op jit(solution)/shard_map/reduce_scatter | solution.py:104
  421.5 1.5 copy-start.15
  427.1 7.3 %copy-start.25 = (f32[1280]{0:T(1024)S(1)}, f32[1280]{0:T(1024)}, u32[]{:S(2)}) copy-start(f32[1280]{0:T(1024)} %copy-done.23) | copy-start | bytes 15364
  427.1 7.3 %copy-start.31 = (f32[1280]{0:T(1024)S(1)}, f32[1280]{0:T(1024)}, u32[]{:S(2)}) copy-start(f32[1280]{0:T(1024)} %copy-done.29) | copy-start | bytes 15364
  427.1 7.3 %copy-start.38 = (f32[1024]{0:T(1024)S(1)}, f32[1024]{0:T(1024)}, u32[]{:S(2)}) copy-start(f32[1024]{0:T(1024)} %param.24) | copy-start | bytes 12292
  427.2 7.3 %copy-start.50 = (f32[1024]{0:T(1024)S(1)}, f32[1024]{0:T(1024)}, u32[]{:S(2)}) copy-start(f32[1024]{0:T(1024)} %param.25) | copy-start | bytes 12292
  427.2 254.4 %all-reduce.13.cloned.1.call-start = ((), (), s32[]{:S(2)}) async-start(), calls=%async_computation.7 | async-start | bytes 12582912 | tf_op jit(solution)/shard_map/psum | solution.py:169
  427.4 7.1 %copy-start.52 = (bf16[1280,1024]{1,0:T(8,128)(2,1)S(1)}, bf16[1280,1024]{1,0:T(8,128)(2,1)}, u32[]{:S(2)}) copy-start(bf16[1280,1024]{1,0:T(8,128)(2,1)} %copy-done.51) | copy-start | bytes 7864324
  427.4 14.4 %slice-start.2 = ((s8[5242880]{0:T(1024)(128)(4,1)}), s8[4194304]{0:T(1024)(128)(4,1)S(1)}, s32[]{:S(2)}) async-start(s8[5242880]{0:T(1024)(128)(4,1)} %bitcast.97), calls=%async_computation.10 | async-start | bytes 8388608
  434.5 7.3 %slice-start.3 = ((s8[5242880]{0:T(1024)(128)(4,1)}), s8[1048576]{0:T(1024)(128)(4,1)S(1)}, s32[]{:S(2)}) async-start(s8[5242880]{0:T(1024)(128)(4,1)} %bitcast.97), calls=%async_computation.11 | async-start | bytes 2097152
  441.8 1.8 copy-start.14
  441.8 2.6 copy-start.19
  447.8 0.8 copy-start.33
  447.8 0.9 copy-start.27
  447.8 73.6 %copy-start.40 = (f32[1024]{0:T(1024)S(1)}, f32[1024]{0:T(1024)}, u32[]{:S(2)}) copy-start(f32[1024]{0:T(1024)} %param.18) | copy-start | bytes 12292
  521.4 7.5 %copy-start.41 = (bf16[1024]{0:T(1024)(128)(2,1)S(1)}, bf16[1024]{0:T(1024)(128)(2,1)}, u32[]{:S(2)}) copy-start(bf16[1024]{0:T(1024)(128)(2,1)} %get-tuple-element.35) | copy-start | bytes 6148
  521.4 7.5 %copy-start.42 = (bf16[1024]{0:T(1024)(128)(2,1)S(1)}, bf16[1024]{0:T(1024)(128)(2,1)}, u32[]{:S(2)}) copy-start(bf16[1024]{0:T(1024)(128)(2,1)} %get-tuple-element.46) | copy-start | bytes 6148
  521.4 7.5 %copy-start.43 = (bf16[1024]{0:T(1024)(128)(2,1)S(1)}, bf16[1024]{0:T(1024)(128)(2,1)}, u32[]{:S(2)}) copy-start(bf16[1024]{0:T(1024)(128)(2,1)} %get-tuple-element.14) | copy-start | bytes 6148
  521.4 7.5 %copy-start.47 = (bf16[1024]{0:T(1024)(128)(2,1)S(1)}, bf16[1024]{0:T(1024)(128)(2,1)}, u32[]{:S(2)}) copy-start(bf16[1024]{0:T(1024)(128)(2,1)} %get-tuple-element.32) | copy-start | bytes 6148
  681.6 5.8 copy-start.17
  683.9 6.0 copy-start.16
Sparse Core Ops, SparseCore 0:
  9.6 57.5 all-gather.2
  68.7 52.9 all-gather.4
  124.7 102.2 all-reduce.6
  261.0 103.0 all-reduce.8
  416.1 103.0 all-reduce.10
  521.9 51.2 reduce-scatter.1
  578.0 103.5 all-reduce.12
where the time goes:
time: 709 us; the launch traced here: 699 us
  waiting for transfers between devices  459 us (65%)
  matrix products  80.7 us (11%)
  other arithmetic  67.8 us (10%)
  local copies, waits for them, and re-layouts  51.3 us (7%)
  blocking collectives  24.7 us (3%)
  between operations  15.1 us (2%)
    psum x1, waiting for transfers between devices, per_device(): lax.psum(attn_part.astype(jnp.bfloat16), 'tensor').astype(jnp.float32)  105 us
    psum x1, waiting for transfers between devices, per_device(): lax.psum(grad_w_qkv.astype(jnp.bfloat16), 'dp').astype(jnp.float32)  104 us
    psum x1, waiting for transfers between devices, per_device(): lax.psum(hidden_part.astype(jnp.bfloat16), 'tensor').astype(jnp.float32)  102 us
    psum x1, waiting for transfers between devices, per_device(): lax.psum(normed_part.astype(jnp.bfloat16), 'tensor').astype(jnp.float32)  67.9 us
    all_gather x1, waiting for transfers between devices, per_device(): lax.all_gather(images, 'tensor', axis=2, tiled=True)  54.3 us
    psum x1, blocking collectives, per_device(): lax.psum(grad_norm1_gain.astype(jnp.bfloat16), 'dp').astype(jnp.float32)  24.7 us
    unnamed x118, local copies, waits for them, and re-layouts  20.9 us
    dot_general x1, matrix products, per_device(): jnp.einsum('rd,fd->rf', grad_ff, w_fc2, preferred_element_type=jnp.float32)  16.8 us
  transfers between devices with their start and end apart: 7, of which 7 were waited for; matrix products, arithmetic and copies ran while one was open for 14% of the time, Pallas kernels for 0%

commit v1 on v0

--- a/solution.py
+++ b/solution.py
@@ -6,6 +6,34 @@
 HEAD_DIM = 64
 EPS = 1e-06
 MASKED = -1e30
+
+
+def grid_tell(payload, where_dim):
+    earlier, state_next, known = (
+        lax.axis_size("tensor"),
+        lax.axis_index("tensor"),
+        payload.shape[where_dim],
+    )
+    grid = [pp * earlier if p == where_dim else pp for p, pp in enumerate(payload.shape)]
+    r1 = lax.dynamic_update_slice_in_dim(
+        jnp.zeros(grid, payload.dtype), payload, state_next * known, axis=where_dim
+    )
+    newest = left_arr = payload
+    for to_i in range(1, earlier // 2 + 1):
+        newest = lax.ppermute(
+            newest, axis_name="tensor", perm=[(p, (p + 1) % earlier) for p in range(earlier)]
+        )
+        r1 = lax.dynamic_update_slice_in_dim(
+            r1, newest, (state_next - to_i) % earlier * known, axis=where_dim
+        )
+        if 2 * to_i < earlier:
+            left_arr = lax.ppermute(
+                left_arr, axis_name="tensor", perm=[(p, (p - 1) % earlier) for p in range(earlier)]
+            )
+            r1 = lax.dynamic_update_slice_in_dim(
+                r1, left_arr, (state_next + to_i) % earlier * known, axis=where_dim
+            )
+    return r1
 
 
 def norm_rows(values, gain_row, shift_row):
@@ -61,7 +89,7 @@
     score_scale = HEAD_DIM ** (-0.5)
     first_col = lax.axis_index("tensor") * col_count
     full_images, full_cot = (
-        lax.all_gather(images, "tensor", axis=2, tiled=True),
+        grid_tell(images, 2),
         lax.all_gather(cotangent, "tensor", axis=2, tiled=True),
     )
     slot_ids = jnp.arange(slot_count, dtype=jnp.int32)

time: 709 us -> 725 us (1.023)
  starting transfers between devices: 0.45 us -> 20.2 us
    ppermute x0 -> x3, waiting for transfers between devices: none -> 54.8 us  [the longest x2 36.4 us: grid_tell(): lax.ppermute(newest, axis_name='tensor', perm=[(p, (p + 1) % earlier) for...]
    all_gather x1 -> x0, waiting for transfers between devices: 54.3 us -> none  [per_device(): lax.all_gather(images, 'tensor', axis=2, tiled=True)]
    ppermute x0 -> x3, starting transfers between devices: none -> 19.8 us  [the longest x2 17.7 us: grid_tell(): lax.ppermute(newest, axis_name='tensor', perm=[(p, (p + 1) % earlier) for...]
    all_gather x1, waiting for transfers between devices: 9.45 us -> 0.01 us  [per_device(): lax.all_gather(cotangent, 'tensor', axis=2, tiled=True)]
    psum x1, waiting for transfers between devices: 105 us -> 114 us  [per_device(): lax.psum(attn_part.astype(jnp.bfloat16), 'tensor').astype(jnp.float32)]
    unnamed x118 -> x122, local copies, waits for them, and re-layouts: 20.9 us -> 20.9 us
  transfers between devices with their start and end apart: 7 -> 9, of which waited for: 7 -> 8; matrix products, arithmetic and copies ran while one was open for 14% -> 14% of each run, Pallas kernels for 0% -> 0%
where the time goes in v1:
time: 725 us; the launch traced here: 715 us
  waiting for transfers between devices  457 us (63%)
  matrix products  80.7 us (11%)
  other arithmetic  63.6 us (9%)
  local copies, waits for them, and re-layouts  54.1 us (7%)
  blocking collectives  24.7 us (3%)
  starting transfers between devices  20.2 us (3%)
  between operations  15.2 us (2%)
    psum x1, waiting for transfers between devices, per_device(): lax.psum(attn_part.astype(jnp.bfloat16), 'tensor').astype(jnp.float32)  114 us
    psum x1, waiting for transfers between devices, per_device(): lax.psum(grad_w_qkv.astype(jnp.bfloat16), 'dp').astype(jnp.float32)  104 us
    psum x1, waiting for transfers between devices, per_device(): lax.psum(hidden_part.astype(jnp.bfloat16), 'tensor').astype(jnp.float32)  102 us
    psum x1, waiting for transfers between devices, per_device(): lax.psum(normed_part.astype(jnp.bfloat16), 'tensor').astype(jnp.float32)  67.9 us
    ppermute x2, waiting for transfers between devices, grid_tell(): lax.ppermute(newest, axis_name='tensor', perm=[(p, (p + 1) % earlier) for...  36.4 us
    psum x1, blocking collectives, per_device(): lax.psum(grad_norm1_gain.astype(jnp.bfloat16), 'dp').astype(jnp.float32)  24.7 us
    unnamed x122, local copies, waits for them, and re-layouts  20.9 us
    ppermute x1, waiting for transfers between devices, grid_tell(): lax.ppermute(left_arr, axis_name='tensor', perm=[(p, (p - 1) % earlier) f...  18.4 us
  transfers between devices with their start and end apart: 9, of which 8 were waited for; matrix products, arithmetic and copies ran while one was open for 14% of the time, Pallas kernels for 0%

profile of v1, /device:TPU:0, one launch (start us, length us, event | category | flops | bytes accessed | tf_op | source)
XLA Modules:
  0.0 715.5 jit_solution(12717274317932664705)
XLA Ops:
  7.3 3.1 collective-permute-start
  10.4 2.1 collective-permute-start.1
  13.3 18.4 %collective-permute-done = bf16[4,320,256]{2,1,0:T(8,128)(2,1)S(1)} collective-permute-done((bf16[4,320,256]{2,1,0:T(8,128)(2,1)}, bf16[4,320,256]{2,1,0:T(8,128)(2,1)S(1)}, u32[]{:S(2)}, u32[]{:S(2)}) %collective-permute-start) | collective-permute-done | bytes 655392 | tf_op jit(solution)/shard_map/ppermute | solution.py:23
  31.7 14.6 %collective-permute-start.2 = (bf16[4,320,256]{2,1,0:T(8,128)(2,1)S(1)}, bf16[4,320,256]{2,1,0:T(8,128)(2,1)}, u32[]{:S(2)}, u32[]{:S(2)}) collective-permute-start(bf16[4,320,256]{2,1,0:T(8,128)(2,1)S(1)} %collective-permute-done), channel_id=1, source_target_pairs={{0,1},{1,2},{2,3},{3,0},{4,5},{5,6},{6,7},{7,4},{8,9},{9,10},{10,1... | collective-permute-start | bytes 1966088 | tf_op jit(solution)/shard_map/ppermute | solution.py:23
  46.3 2.6 copy.39
  49.5 18.4 %collective-permute-done.1 = bf16[4,320,256]{2,1,0:T(8,128)(2,1)} collective-permute-done((bf16[4,320,256]{2,1,0:T(8,128)(2,1)}, bf16[4,320,256]{2,1,0:T(8,128)(2,1)}, u32[]{:S(2)}, u32[]{:S(2)}) %collective-permute-start.1) | collective-permute-done | bytes 655392 | tf_op jit(solution)/shard_map/ppermute | solution.py:30
  67.9 1.2 constant_dynamic-update-slice_fusion.1
  69.1 18.0 %collective-permute-done.2 = bf16[4,320,256]{2,1,0:T(8,128)(2,1)} collective-permute-done((bf16[4,320,256]{2,1,0:T(8,128)(2,1)S(1)}, bf16[4,320,256]{2,1,0:T(8,128)(2,1)}, u32[]{:S(2)}, u32[]{:S(2)}) %collective-permute-start.2) | collective-permute-done | bytes 655392 | tf_op jit(solution)/shard_map/ppermute | solution.py:23
  87.1 1.2 constant_dynamic-update-slice_fusion
  90.1 1.3 add_convert_fusion.2
  91.4 1.4 copy-done.13
  92.9 3.5 add_convert_fusion.3
  96.4 6.7 reshape.265
  103.1 3.9 fusion.57
  107.0 2.3 copy.64
  109.3 2.5 copy.65
  111.8 3.2 copy.66
  115.0 3.2 fusion.24
  118.2 1.9 fusion
  120.2 2.4 fusion.35
  122.7 1.5 copy.45
  124.1 2.0 reshape.257
  126.2 3.4 convolution_convert_fusion.1
  129.7 114.1 %all-reduce.7.cloned.1.call-done = bf16[1280,1024]{1,0:T(8,128)(2,1)} async-done(((bf16[1280,1024]{1,0:T(8,128)(2,1)}), bf16[1280,1024]{1,0:T(8,128)(2,1)}) %all-reduce.7.cloned.1.call-update) | async-done | bytes 2621456 | tf_op jit(solution)/shard_map/psum | solution.py:124
  243.8 5.0 fusion.56
  249.6 2.5 copy-done.50
  252.1 3.0 fusion.51
  255.2 16.8 %fusion.52 = (bf16[1024]{0:T(1024)(128)(2,1)}, bf16[1280,1024]{1,0:T(8,128)(2,1)S(1)}, f32[1280,1024]{1,0:T(8,128)}) fusion(f32[1280,1024]{1,0:T(8,128)S(1)} %fusion.51, f32[1024]{0:T(1024)S(1)} %copy-done.46, bf16[1280,1024]{1,0:T(8,128)(2,1)S(1)} %get-tuple-element.49, bf16[1024,1024]{1,0:T(8,128)(2,1)S(1)} %copy-done), kind=kOutput, calls=%fused_computation.117 | convolution fusion | flops 2781346816 | bytes 17831936 | tf_op jit(solution)/shard_map/rd,fd->rf/dot_general | solution.py:143
  272.0 1.5 copy-done.53
  273.4 4.2 convolution_convert_fusion.2
  277.7 1.4 log_add_fusion
  279.1 101.8 %all-reduce.9.cloned.1.call-done = bf16[1280,1024]{1,0:T(8,128)(2,1)} async-done(((bf16[1280,1024]{1,0:T(8,128)(2,1)}), bf16[1280,1024]{1,0:T(8,128)(2,1)}) %all-reduce.9.cloned.1.call-update) | async-done | bytes 2621456 | tf_op jit(solution)/shard_map/psum | solution.py:149
  380.9 5.5 fusion.9
  386.4 5.6 convert_reduce_fusion
  392.0 2.3 copy-done.4
  394.3 1.7 convolution_convert_fusion.4
  396.0 3.1 reshape.266
  399.1 3.2 copy.47
  402.3 5.5 fusion.27
  407.9 5.4 multiply_reduce_fusion
  413.3 2.9 multiply_convert_fusion
  416.3 1.3 multiply_bitcast_fusion
  419.0 3.2 copy.52
  422.3 4.7 convert_element_type.226
  427.0 5.7 convolution_convert_fusion
  432.8 5.5 multiply_convert_fusion.2
  438.3 1.5 copy-done.15
  439.8 4.1 convolution_convert_fusion.3
  444.2 7.0 convolution_convert_fusion.5
  451.3 7.3 %convolution_convert_fusion.6 = bf16[1024,1024]{1,0:T(8,128)(2,1)} fusion(bf16[1280,1024]{1,0:T(8,128)(2,1)S(1)} %copy-done.54, f32[1280,1024]{1,0:T(8,128)} %copy-done.2, f32[1024]{0:T(1024)S(1)} %copy-done.52, f32[1024]{0:T(1024)S(1)} %copy-done.39, f32[1280]{0:T(1024)S(1)} %copy-done.32, f32[1280]{0:T(1024)S(1)} %copy-done.26), kind=kOutput, calls=%fused_computation.67 | convolution fusion | flops 2691956736 | bytes 9979904 | tf_op jit(solution)/shard_map/rd,rf->df/dot_general | solution.py:147
  458.6 1.6 convolution_convert_fusion.8
  461.2 3.4 convolution_convert_fusion.7
  465.6 2.4 fusion.25
  468.1 67.9 %all-reduce.11.cloned.1.call-done = bf16[1280,1024]{1,0:T(8,128)(2,1)} async-done(((bf16[1280,1024]{1,0:T(8,128)(2,1)}), bf16[1280,1024]{1,0:T(8,128)(2,1)}) %all-reduce.11.cloned.1.call-update) | async-done | bytes 2621456 | tf_op jit(solution)/shard_map/psum | solution.py:188
  536.0 2.2 reduce_sum.188
  538.3 7.4 %fusion.10 = (bf16[1024]{0:T(1024)(128)(2,1)S(1)}, f32[1280]{0:T(1024)S(1)}, f32[1280]{0:T(1024)S(1)}, f32[1280,1024]{1,0:T(8,128)}, f32[1280,1024]{1,0:T(8,128)}) fusion(bf16[1280,1024]{1,0:T(8,128)(2,1)} %all-reduce.11.cloned.1.call-done, f32[1280]{0:T(1024)S(1)} %rsqrt.22, f32[1280]{0:T(1024)S(1)} %div.43, f32[1280]{0:T(1024)S(1)} %reshape.262, ...), kind=kLoop, calls=%fused_computation.21 | loop fusion | flops 14414336 | bytes 15760384 | tf_op jit(solution)/shard_map/reduce_sum | solution.py:189
  545.7 24.7 %all-reduce = (bf16[1024]{0:T(1024)(128)(2,1)S(1)}, bf16[1024]{0:T(1024)(128)(2,1)S(1)}, bf16[2,256]{1,0:T(2,128)(2,1)S(1)}, bf16[1024]{0:T(1024)(128)(2,1)S(1)}...) all-reduce(bf16[1024]{0:T(1024)(128)(2,1)S(1)} %get-tuple-element.1, ...), channel_id=1, replica_groups=mesh['dp'=8,'tensor'=4] {'dp'}, use_global_device_ids=true, to_apply=%region_16.17 | all-reduce | flops 7680 | bytes 30720 | tf_op jit(solution)/shard_map/psum | solution.py:195
  575.2 14.9 %reduce-scatter.2.cloned.1.call-done = bf16[1280,256]{1,0:T(8,128)(2,1)} async-done(((bf16[1280,1024]{1,0:T(8,128)(2,1)}), bf16[1280,256]{1,0:T(8,128)(2,1)}) %reduce-scatter.2.cloned.1.call-update) | async-done | bytes 655376 | tf_op jit(solution)/shard_map/reduce_scatter | solution.py:132
  590.0 4.1 fusion.32
  594.1 103.6 %all-reduce.13.cloned.1.call-done = (bf16[1024,3,256]{2,0,1:T(8,128)(2,1)}, bf16[256,1024]{1,0:T(8,128)(2,1)}, bf16[1024,1024]{1,0:T(8,128)(2,1)}, bf16[1024,1024]{1,0:T(8,128)(2,1)}) async-done(((bf16[1024,3,256]{2,0,1:T(8,128)(2,1)}, bf16[256,1024]{1,0:T(8,128)(2,1)}, bf16[1024,1024]{1,0:T(8,128)(2,1)}, bf16[1024,1024]{1,0:T(8,128)(2,1)}), (bf16[1024,3,256]{2,0,1:T(8,128)(2,1)}, ...) | async-done | bytes 6291472 | tf_op jit(solution)/shard_map/psum | solution.py:197
  697.7 2.3 convert_element_type.238
  700.0 3.5 convert_element_type.234
  703.5 2.5 convert_element_type.244
  705.9 2.5 convert_element_type.247
  (163 shorter events, 12.8 us)
Async XLA Ops:
  7.2 248.0 %copy-start = (bf16[1024,1024]{1,0:T(8,128)(2,1)S(1)}, bf16[1024,1024]{1,0:T(8,128)(2,1)}, u32[]{:S(2)}) copy-start(bf16[1024,1024]{1,0:T(8,128)(2,1)} %param.28) | copy-start | bytes 6291460
  7.2 42.1 %copy-start.21 = (bf16[4,320,256]{2,1,0:T(8,128)(2,1)S(1)}, bf16[4,320,256]{2,1,0:T(8,128)(2,1)}, u32[]{:S(2)}) copy-start(bf16[4,320,256]{2,1,0:T(8,128)(2,1)} %param.15) | copy-start | bytes 1966084
  7.2 42.2 %copy-start.49 = (s32[4]{0:T(128)S(1)}, s32[4]{0:T(128)}, u32[]{:S(2)}) copy-start(s32[4]{0:T(128)} %param.16) | copy-start | bytes 52
  7.2 122.5 %all-gather.2.cloned.1.call-start = ((), (), s32[]{:S(2)}) async-start(), calls=%async_computation.3 | async-start | bytes 3276800 | tf_op jit(solution)/shard_map/all_gather | solution.py:93
  7.3 24.4 %collective-permute-start = (bf16[4,320,256]{2,1,0:T(8,128)(2,1)}, bf16[4,320,256]{2,1,0:T(8,128)(2,1)S(1)}, u32[]{:S(2)}, u32[]{:S(2)}) collective-permute-start(bf16[4,320,256]{2,1,0:T(8,128)(2,1)} %param.15), channel_id=1, source_target_pairs={{0,1},{1,2},{2,3},{3,0},{4,5},{5,6},{6,7},{7,4},{8,9},{9,10},{10,1... | collective-permute-start | bytes 1966088 | tf_op jit(solution)/shard_map/ppermute | solution.py:23
  10.4 57.5 %collective-permute-start.1 = (bf16[4,320,256]{2,1,0:T(8,128)(2,1)}, bf16[4,320,256]{2,1,0:T(8,128)(2,1)}, u32[]{:S(2)}, u32[]{:S(2)}) collective-permute-start(bf16[4,320,256]{2,1,0:T(8,128)(2,1)} %param.15), channel_id=1, source_target_pairs={{0,3},{1,0},{2,1},{3,2},{4,7},{5,4},{6,5},{7,6},{8,11},{9,8},{10,9... | collective-permute-start | bytes 1966088 | tf_op jit(solution)/shard_map/ppermute | solution.py:30
  12.5 231.3 %all-reduce.7.cloned.1.call-start = ((), (), s32[]{:S(2)}) async-start(), calls=%async_computation.1 | async-start | bytes 5242880 | tf_op jit(solution)/shard_map/psum | solution.py:124
  31.7 55.4 %collective-permute-start.2 = (bf16[4,320,256]{2,1,0:T(8,128)(2,1)S(1)}, bf16[4,320,256]{2,1,0:T(8,128)(2,1)}, u32[]{:S(2)}, u32[]{:S(2)}) collective-permute-start(bf16[4,320,256]{2,1,0:T(8,128)(2,1)S(1)} %collective-permute-done), channel_id=1, source_target_pairs={{0,1},{1,2},{2,3},{3,0},{4,5},{5,6},{6,7},{7,4},{8,9},{9,10},{10,1... | collective-permute-start | bytes 1966088 | tf_op jit(solution)/shard_map/ppermute | solution.py:23
  49.3 40.8 %copy-start.40 = (f32[1024]{0:T(1024)S(1)}, f32[1024]{0:T(1024)}, u32[]{:S(2)}) copy-start(f32[1024]{0:T(1024)} %param.18) | copy-start | bytes 12292
  49.3 40.8 %copy-start.45 = (f32[1024]{0:T(1024)S(1)}, f32[1024]{0:T(1024)}, u32[]{:S(2)}) copy-start(f32[1024]{0:T(1024)} %param.19) | copy-start | bytes 12292
  49.5 70.7 %copy-start.35 = (pred[4,320]{1,0:T(4,128)(4,1)}, pred[4,320]{1,0:T(4,128)(4,1)S(1)}, u32[]{:S(2)}) copy-start(pred[4,320]{1,0:T(4,128)(4,1)S(1)} %get-tuple-element.54) | copy-start | bytes 3844
  88.3 3.1 copy-start.3
  88.3 4.6 copy-start.20
  89.0 2.4 copy-start.27
  90.1 1.4 copy-start.33
  91.4 1.5 copy-start.13
  118.2 4.4 copy-start.1
  118.2 4.4 copy-start.23
  118.2 1.9 copy-start.9
  120.2 2.5 copy-start.29
  129.6 251.3 %all-reduce.9.cloned.1.call-start = ((), (), s32[]{:S(2)}) async-start(), calls=%async_computation.4 | async-start | bytes 5242880 | tf_op jit(solution)/shard_map/psum | solution.py:149
  248.8 6.3 copy-start.2
  248.8 6.3 copy-start.12
  248.8 3.2 copy-start.50
  248.8 3.2 copy-start.51
  248.9 6.2 copy-start.24
  252.1 3.1 copy-start.30
  252.1 3.1 copy-start.46
  255.1 16.8 %copy-start.8 = (f32[1280,1024]{1,0:T(8,128)}, f32[1280,1024]{1,0:T(8,128)S(1)}, u32[]{:S(2)}) copy-start(f32[1280,1024]{1,0:T(8,128)S(1)} %fusion.51) | copy-start | bytes 15728644
  272.0 1.5 copy-start.53
  277.7 258.4 %all-reduce.11.cloned.1.call-start = ((), (), s32[]{:S(2)}) async-start(), calls=%async_computation.5 | async-start | bytes 5242880 | tf_op jit(solution)/shard_map/psum | solution.py:188
  380.9 5.5 copy-start.5
  380.9 5.5 copy-start.6
  380.9 5.5 copy-start.25
  380.9 5.5 copy-start.31
  380.9 5.5 copy-start.38
  386.4 7.8 %copy-start.18 = (bf16[256,1024]{1,0:T(8,128)(2,1)S(1)}, bf16[256,1024]{1,0:T(8,128)(2,1)}, u32[]{:S(2)}) copy-start(bf16[256,1024]{1,0:T(8,128)(2,1)} %param.22) | copy-start | bytes 1572868
  392.0 2.3 copy-start.4
  402.3 5.5 copy-start.10
  402.3 5.6 copy-start.11
  402.3 5.6 copy-start.22
  402.3 5.6 copy-start.36
  402.3 11.0 %slice-start = ((s8[7864320]{0:T(1024)(128)(4,1)}), s8[4194304]{0:T(1024)(128)(4,1)S(1)}, s32[]{:S(2)}) async-start(s8[7864320]{0:T(1024)(128)(4,1)} %bitcast.95), calls=%async_computation.7 | async-start | bytes 8388608
  407.9 5.4 slice-start.1
  427.0 5.8 copy-start.47
  432.8 157.3 %reduce-scatter.2.cloned.1.call-start = ((), (), s32[]{:S(2)}) async-start(), calls=%async_computation.2 | async-start | bytes 3276800 | tf_op jit(solution)/shard_map/reduce_scatter | solution.py:132
  438.3 1.5 copy-start.15
  443.9 7.3 %copy-start.26 = (f32[1280]{0:T(1024)S(1)}, f32[1280]{0:T(1024)}, u32[]{:S(2)}) copy-start(f32[1280]{0:T(1024)} %copy-done.24) | copy-start | bytes 15364
  443.9 7.3 %copy-start.32 = (f32[1280]{0:T(1024)S(1)}, f32[1280]{0:T(1024)}, u32[]{:S(2)}) copy-start(f32[1280]{0:T(1024)} %copy-done.30) | copy-start | bytes 15364
  444.0 7.3 %copy-start.39 = (f32[1024]{0:T(1024)S(1)}, f32[1024]{0:T(1024)}, u32[]{:S(2)}) copy-start(f32[1024]{0:T(1024)} %param.24) | copy-start | bytes 12292
  444.0 7.3 %copy-start.52 = (f32[1024]{0:T(1024)S(1)}, f32[1024]{0:T(1024)}, u32[]{:S(2)}) copy-start(f32[1024]{0:T(1024)} %param.25) | copy-start | bytes 12292
  444.0 253.7 %all-reduce.13.cloned.1.call-start = ((), (), s32[]{:S(2)}) async-start(), calls=%async_computation.6 | async-start | bytes 12582912 | tf_op jit(solution)/shard_map/psum | solution.py:197
  444.2 7.1 copy-start.54
  444.2 14.4 %slice-start.2 = ((s8[5242880]{0:T(1024)(128)(4,1)}), s8[4194304]{0:T(1024)(128)(4,1)S(1)}, s32[]{:S(2)}) async-start(s8[5242880]{0:T(1024)(128)(4,1)} %bitcast.97), calls=%async_computation.9 | async-start | bytes 8388608
  451.3 7.3 %slice-start.3 = ((s8[5242880]{0:T(1024)(128)(4,1)}), s8[1048576]{0:T(1024)(128)(4,1)S(1)}, s32[]{:S(2)}) async-start(s8[5242880]{0:T(1024)(128)(4,1)} %bitcast.97), calls=%async_computation.10 | async-start | bytes 2097152
  458.6 1.8 copy-start.14
  458.6 2.6 copy-start.19
  464.6 73.6 %copy-start.41 = (f32[1024]{0:T(1024)S(1)}, f32[1024]{0:T(1024)}, u32[]{:S(2)}) copy-start(f32[1024]{0:T(1024)} %param.18) | copy-start | bytes 12292
  538.2 7.5 %copy-start.42 = (bf16[1024]{0:T(1024)(128)(2,1)S(1)}, bf16[1024]{0:T(1024)(128)(2,1)}, u32[]{:S(2)}) copy-start(bf16[1024]{0:T(1024)(128)(2,1)} %get-tuple-element.35) | copy-start | bytes 6148
  538.2 7.5 %copy-start.43 = (bf16[1024]{0:T(1024)(128)(2,1)S(1)}, bf16[1024]{0:T(1024)(128)(2,1)}, u32[]{:S(2)}) copy-start(bf16[1024]{0:T(1024)(128)(2,1)} %get-tuple-element.46) | copy-start | bytes 6148
  538.2 7.5 %copy-start.44 = (bf16[1024]{0:T(1024)(128)(2,1)S(1)}, bf16[1024]{0:T(1024)(128)(2,1)}, u32[]{:S(2)}) copy-start(bf16[1024]{0:T(1024)(128)(2,1)} %get-tuple-element.14) | copy-start | bytes 6148
  538.3 7.5 %copy-start.48 = (bf16[1024]{0:T(1024)(128)(2,1)S(1)}, bf16[1024]{0:T(1024)(128)(2,1)}, u32[]{:S(2)}) copy-start(bf16[1024]{0:T(1024)(128)(2,1)} %get-tuple-element.32) | copy-start | bytes 6148
  697.7 5.8 copy-start.17
  700.0 6.0 copy-start.16
  (4 other events, 3.8 us)
Sparse Core Ops, SparseCore 0:
  12.6 85.1 all-gather.1
  129.7 114.0 all-reduce.6
  277.8 103.0 all-reduce.8
  432.9 103.0 all-reduce.10
  538.7 51.2 reduce-scatter.1
  594.1 103.5 all-reduce.12
